TPU v7x, 32 devices: a whole 2x2x4 slice. The times are simulated.
32 devices in a mesh: group: 4 (over y, x), expert: 4 (over z), dp: 2 (over core).
Axes of the slice: x: 2, y: 2, z: 4, core: 2. Of those that a mesh axis runs over, the one named last changes fastest.
Arguments:
- tokens: bfloat16 [8, 16, 7168], P(('expert', 'dp'), 'group'), may hold values from -6 to 6
- expert_ids: int32 [8, 16, 8], P(('expert', 'dp')), may hold values from 0 to 31, as said below
- gate_codes: int32 [8, 16, 8], P(('expert', 'dp')), may hold values from 1 to 1023
- w_gate: bfloat16 [4, 7168, 2048], P('expert', None, 'group'), may hold values from -0.0625 to 0.0625
- w_up: bfloat16 [4, 7168, 2048], P('expert', None, 'group'), may hold values from -0.0625 to 0.0625
- w_down: bfloat16 [4, 2048, 7168], P('expert', 'group'), may hold values from -0.125 to 0.125
Outputs:
- mixed: bfloat16 [8, 16, 7168], P(('expert', 'dp'), 'group')
Inputs may be any that keep to these rules, and one draw needn't show every extreme that they name: `expert_ids`: each token names 8 different experts, all within at most 4 of the 8 groups of 4 consecutive ids. In every set (one index of the first dimension), each expert below 4 is named by at most 4 tokens, and some expert by exactly 4; a token names at most 4 experts below 4.
All inputs are finite; a program needn't handle non-finite values.
Results may differ from a plain program's by a relative error of at most 0.015.
Values may be sent and summed in bfloat16 or wider, within the bound.
A program may use at most 64 MiB of HBM per device.

v0:
```python
import functools

import jax
import jax.numpy as jnp
from jax import lax
from jax.experimental import pallas as pl
from jax.experimental.pallas import tpu as pltpu
from jax.sharding import PartitionSpec as P

CAPG = 4
FORWARD = (1, 1, 1, 1)
BACK = (1, 1, 1, 1)
MESH = pl.DeviceIdType.MESH


def dot(a, b):
    return jnp.dot(a, b, preferred_element_type=jnp.float32)


def routing(ids, codes, experts, capacity):
    tokens = ids.shape[1]
    wide = experts * capacity
    codes = codes.astype(jnp.float32)
    gates = 2.5 * codes / jnp.sum(codes, axis=0, keepdims=True)
    slot = lax.broadcasted_iota(jnp.int32, (wide, tokens), 0)
    member = jnp.zeros((wide, tokens), jnp.float32)
    weight = jnp.zeros((wide, tokens), jnp.float32)
    for e in range(experts):
        hits = ids == e
        named = jnp.max(jnp.where(hits, 1.0, 0.0), axis=0, keepdims=True)
        gate = jnp.sum(jnp.where(hits, gates, 0.0), axis=0, keepdims=True)
        mine = (slot >= e * capacity) & (slot < (e + 1) * capacity)
        member = jnp.where(mine, named, member)
        weight = jnp.where(mine, gate, weight)
    row = lax.broadcasted_iota(jnp.int32, (tokens, tokens), 0)
    column = lax.broadcasted_iota(jnp.int32, (tokens, tokens), 1)
    before = jnp.where(row < column, 1.0, 0.0).astype(jnp.bfloat16)
    rank = dot(member.astype(jnp.bfloat16), before)
    place = jnp.where(rank == (slot % capacity).astype(jnp.float32), member, 0.0)
    mix = place * weight
    high = mix.astype(jnp.bfloat16)
    low = (mix - high.astype(jnp.float32)).astype(jnp.bfloat16)
    return place.astype(jnp.bfloat16), jnp.concatenate([flipped(high), flipped(low)], axis=0)


def flipped(a):
    n = a.shape[1]
    row = lax.broadcasted_iota(jnp.int32, (n, n), 0)
    column = lax.broadcasted_iota(jnp.int32, (n, n), 1)
    eye = jnp.where(row == column, 1.0, 0.0).astype(jnp.bfloat16)
    return lax.dot_general(
        eye, a, (((1,), (1,)), ((), ())), preferred_element_type=jnp.float32
    ).astype(jnp.bfloat16)


def pieces(width, shares):
    ends = [0]
    for k in range(len(shares)):
        ends.append(width * sum(shares[: k + 1]) // sum(shares) // 128 * 128)
    return [pl.ds(a, b - a) for a, b in zip(ends[:-1], ends[1:])]


def partner(a, m, n):
    out, bit = 0, 1
    while bit < n:
        out = out + bit * lax.rem(lax.div(a, bit) + m // bit % 2, 2)
        bit *= 2
    return out


def kernel(
    groups, experts, sets, tokens, ids, codes, w_gate, w_up, w_down, red,
    tok, named, wgu, wd, rows, slots, acc, part, ret, mixed,
    tok_sem, in_sem, w_sem, d_sem, id_s, id_r, ga_s, ga_r, di_s, di_r, re_s, re_r, sc_s, sc_r, go,
):
    g = lax.axis_index("group")
    z = lax.axis_index("expert")
    d = lax.axis_index("dp")
    lead = sets - 1
    own, width = tokens.shape
    cuts = pieces(width, FORWARD)
    back_cuts = pieces(width, BACK)
    cap = CAPG
    peer = [partner(g, m, groups) for m in range(groups)]
    far = [partner(z, m, experts) for m in range(experts)]
    group_order = list(range(groups - 1, -1, -1))
    expert_order = list(range(experts - 1, -1, -1))
    barrier = pltpu.get_barrier_semaphore()

    tok_in = pltpu.make_async_copy(tokens, tok.at[d, g], tok_sem)
    tok_in.start()
    pltpu.make_async_copy(ids, named.at[d, 0], in_sem).start()
    pltpu.make_async_copy(codes, named.at[d, 1], in_sem).start()
    named_in = pltpu.make_async_copy(named.at[d], named.at[d], in_sem)

    def greet(**to):
        pl.semaphore_signal(barrier, inc=1, device_id=to, device_id_type=MESH)

    def remote(to, src, dst, send, recv):
        return pltpu.make_async_remote_copy(
            src_ref=src, dst_ref=dst, send_sem=send, recv_sem=recv,
            device_id=to, device_id_type=MESH,
        )

    def landed(ref, sem):
        pltpu.make_async_copy(ref, ref, sem).wait()

    def load():
        for c, cut in enumerate(cuts):
            pltpu.make_async_copy(w_gate.at[cut, :], wgu.at[0, cut, :], w_sem.at[c]).start()
            pltpu.make_async_copy(w_up.at[cut, :], wgu.at[1, cut, :], w_sem.at[c]).start()
        for c, cut in enumerate(back_cuts):
            pltpu.make_async_copy(w_down.at[:, cut], wd.at[:, cut], d_sem.at[c]).start()

    def send_tokens(order):
        for cut, sem in zip(cuts, range(len(cuts))):
            for m in order:
                remote(
                    {"group": peer[m], "dp": lead}, tok.at[d, g, :, cut], tok.at[d, g, :, cut],
                    ga_s, ga_r.at[sem, d],
                ).start()

    def compute(present, order):
        for c, cut in enumerate(cuts):
            landed(slots.at[pl.ds(0, present), :, cut], di_r.at[c])
            landed(wgu.at[:, cut, :], w_sem.at[c])
            flat = slots[:, :, cut].reshape(experts * cap, cut.size)
            for i in range(2):
                made = dot(flat, wgu[i, cut, :])
                acc[i] = made if c == 0 else acc[i] + made
        hidden = (acc[0] / (1.0 + jnp.exp(-acc[0])) * acc[1]).astype(jnp.bfloat16)
        for c, cut in enumerate(back_cuts):
            landed(wd.at[:, cut], d_sem.at[c])
            made = dot(hidden, wd[:, cut]).astype(jnp.bfloat16)
            part[:, :, cut] = made.reshape(experts, cap, cut.size)
            for m in order:
                remote(
                    {"expert": far[m], "dp": lead}, part.at[far[m], :, cut], ret.at[d, z, :, cut],
                    re_s, re_r.at[c, d],
                ).start()
            if present < experts:
                ret[lead, z, :, cut] = part[z, :, cut]

    @pl.when(d == lead)
    def _():
        for m in range(1, groups):
            greet(group=peer[m])
        for m in range(1, experts):
            for s in range(lead):
                greet(expert=far[m], dp=s)
        load()
        tok_in.wait()
        pl.semaphore_wait(barrier, groups - 1 + lead)
        for s in range(lead):
            pl.semaphore_signal(go, inc=1, device_id={"dp": s}, device_id_type=MESH)
        send_tokens(group_order[:-1])

        named_in.wait()
        routes = {lead: routing(named[lead, 0], named[lead, 1], experts, cap)}
        for s in range(lead):
            landed(named.at[s], id_r.at[s])
            routes[s] = routing(named[s, 0], named[s, 1], experts, cap)

        for s in range(lead, -1, -1):
            for c, cut in enumerate(cuts):
                landed(tok.at[s, pl.ds(0, groups - 1 if s == lead else groups), :, cut], ga_r.at[c, s])
                chosen = dot(routes[s][0], tok[s, :, :, cut].reshape(groups * own, cut.size))
                rows[s, :, :, cut] = chosen.astype(jnp.bfloat16).reshape(experts, cap, cut.size)
                if (s, c) == (lead, 0):
                    pl.semaphore_wait(go, lead)
                for m in expert_order:
                    if (s, m) != (lead, 0):
                        remote(
                            {"expert": far[m], "dp": s}, rows.at[s, far[m], :, cut], slots.at[z, :, cut],
                            di_s.at[s], di_r.at[c],
                        ).start()
                if s == lead:
                    slots[z, :, cut] = rows[s, z, :, cut]

        compute(experts - 1, expert_order[:-1])

        for s in range(lead, -1, -1):
            for c, cut in enumerate(back_cuts):
                landed(ret.at[s, pl.ds(0, experts - 1 if s == lead else experts), :, cut], re_r.at[c, s])
                both = dot(routes[s][1], ret[s, :, :, cut].reshape(experts * cap, cut.size))
                total = (both[: groups * own] + both[groups * own :]).astype(jnp.bfloat16)
                mixed[s, :, :, cut] = total.reshape(groups, own, cut.size)
                for m in group_order:
                    if (s, m) != (lead, 0):
                        remote(
                            {"group": peer[m], "dp": s}, mixed.at[s, peer[m], :, cut], red.at[g, :, cut],
                            sc_s.at[s], sc_r.at[c],
                        ).start()
                if s == lead:
                    pltpu.make_async_copy(mixed.at[s, g, :, cut], red.at[g, :, cut], sc_r.at[c]).start()

        landed(tok.at[lead, pl.ds(0, groups - 1)], ga_s)
        landed(part.at[pl.ds(0, experts - 1)], re_s)
        for s in range(sets):
            landed(rows.at[s, pl.ds(0, experts - 1 if s == lead else experts)], di_s.at[s])
            landed(mixed.at[s, pl.ds(0, groups - 1 if s == lead else groups)], sc_s.at[s])

    @pl.when(d != lead)
    def _():
        greet(dp=lead)
        for m in range(1, experts):
            greet(expert=far[m])
        load()
        tok_in.wait()
        named_in.wait()
        pl.semaphore_wait(go, 1)
        send_tokens(group_order)
        remote({"dp": lead}, named.at[d], named.at[d], id_s, id_r.at[d]).start()
        pl.semaphore_wait(barrier, 2 * (experts - 1))
        pl.semaphore_signal(go, inc=1, device_id={"dp": lead}, device_id_type=MESH)

        compute(experts, expert_order)

        landed(tok.at[d], ga_s)
        landed(named.at[d], id_s)
        landed(part, re_s)

    for c, cut in enumerate(back_cuts):
        landed(red.at[:, :, cut], sc_r.at[c])


def per_device(tokens, expert_ids, gate_codes, w_gate, w_up, w_down):
    groups = lax.axis_size("group")
    experts = lax.axis_size("expert")
    sets = lax.axis_size("dp")
    own, width = tokens.shape[1:]
    hid = w_gate.shape[2]
    bf16 = jnp.bfloat16
    any_space = pl.BlockSpec(memory_space=pl.ANY)
    dma = pltpu.SemaphoreType.DMA
    shares = pl.pallas_call(
        functools.partial(kernel, groups, experts, sets),
        out_shape=jax.ShapeDtypeStruct((groups, own, width), bf16),
        in_specs=[any_space] * 6,
        out_specs=any_space,
        scratch_shapes=[
            pltpu.VMEM((sets, groups, own, width), bf16),
            pltpu.VMEM((sets, 2, *expert_ids.shape[:0:-1]), jnp.int32),
            pltpu.VMEM((2, width, hid), bf16),
            pltpu.VMEM((hid, width), bf16),
            pltpu.VMEM((sets, experts, CAPG, width), bf16),
            pltpu.VMEM((experts, CAPG, width), bf16),
            pltpu.VMEM((2, experts * CAPG, hid), jnp.float32),
            pltpu.VMEM((experts, CAPG, width), bf16),
            pltpu.VMEM((sets, experts, CAPG, width), bf16),
            pltpu.VMEM((sets, groups, own, width), bf16),
            dma,
            dma,
            dma((len(FORWARD),)),
            dma((len(BACK),)),
            dma,
            dma((sets - 1,)),
            dma,
            dma((len(FORWARD), sets)),
            dma((sets,)),
            dma((len(FORWARD),)),
            dma,
            dma((len(BACK), sets)),
            dma((sets,)),
            dma((len(BACK),)),
            pltpu.SemaphoreType.REGULAR,
        ],
        compiler_params=pltpu.CompilerParams(
            collective_id=0, has_side_effects=True, vmem_limit_bytes=60 * 1024 * 1024
        ),
    )(tokens[0], expert_ids[0].T, gate_codes[0].T, w_gate[0], w_up[0], w_down[0])
    total = shares[0].astype(jnp.float32)
    for k in range(1, groups):
        total = total + shares[k].astype(jnp.float32)
    return total.astype(bf16)[None]


def solution(mesh):
    placed = (
        P(("expert", "dp"), "group", None),
        P(("expert", "dp"), None, None),
        P(("expert", "dp"), None, None),
        P("expert", None, "group"),
        P("expert", None, "group"),
        P("expert", "group", None),
    )
    return jax.shard_map(
        per_device,
        mesh=mesh,
        in_specs=placed,
        out_specs=P(("expert", "dp"), "group", None),
        check_vma=False,
    )
```

profile of v0, /device:TPU:0, one launch (start us, length us, event | category | flops | bytes accessed | tf_op | source)
XLA Modules:
  0.0 24.8 jit_solution(549271470008917649)
XLA Ops:
  0.0 23.2 %shard_map.64 = bf16[4,4,7168]{2,1,0:T(4,128)(2,1)} custom-call(bf16[4,7168]{1,0:T(4,128)(2,1)} %bitcast.13, s32[8,16]{1,0:T(8,128)} %bitcast.14, s32[8,16]{1,0:T(8,128)} %bitcast.15, bf16[7168,512]{1,0:T(8,128)(2,1)} %bitcast.10, bf16[7168,512]{1,0:T(8,128)(2,1)} %bitcast.11, bf16[512,7168]{1,0:T(8,128)(2,1)} %bitcast.12), custom_call_target="tpu_custom_call" | custom-call | tf_op jit(solution)/shard_map/pallas_call | solution.py:236
  23.2 1.6 %add_convert_fusion = bf16[1,4,7168]{2,1,0:T(4,128)(2,1)} fusion(bf16[4,4,7168]{2,1,0:T(4,128)(2,1)} %shard_map.64), kind=kLoop, calls=%fused_computation | loop fusion | flops 229376 | bytes 286720 | tf_op jit(solution)/shard_map/convert_element_type | solution.py:275
where the time goes:
time: 25 us; the launch traced here: 24.8 us
  Pallas kernels  23.2 us (93%)
  other arithmetic  1.59 us (6%)
    pallas_call x1, Pallas kernels, per_device(): pl.pallas_call(functools.partial(kernel, groups, experts, sets), out_shap...  23.2 us
    convert_element_type x1, other arithmetic, per_device(): return total.astype(bf16)[None]  1.59 us

commit v1 on v0

--- a/solution.py
+++ b/solution.py
@@ -8,8 +8,9 @@
 from jax.sharding import PartitionSpec as P
 
 CAPG = 4
-FORWARD = (1, 1, 1, 1)
-BACK = (1, 1, 1, 1)
+FORWARD = (1, 2, 2, 2)
+BACK = (1, 2, 2, 2)
+URGENT = 1
 MESH = pl.DeviceIdType.MESH
 
 
@@ -68,6 +69,12 @@
     return out
 
 
+def ends_first(z, k, n):
+    at = jnp.where(z == 0, 0, jnp.where(z == n - 1, 1, z + 1))
+    i = k + jnp.where(k >= at, 1, 0)
+    return jnp.where(i == 0, 0, jnp.where(i == 1, n - 1, i - 1))
+
+
 def kernel(
     groups, experts, sets, tokens, ids, codes, w_gate, w_up, w_down, red,
     tok, named, wgu, wd, rows, slots, acc, part, ret, mixed,
@@ -85,6 +92,7 @@
     far = [partner(z, m, experts) for m in range(experts)]
     group_order = list(range(groups - 1, -1, -1))
     expert_order = list(range(experts - 1, -1, -1))
+    away = [ends_first(z, k, experts) for k in range(experts - 1)]
     barrier = pltpu.get_barrier_semaphore()
 
     tok_in = pltpu.make_async_copy(tokens, tok.at[d, g], tok_sem)
@@ -120,7 +128,13 @@
                     ga_s, ga_r.at[sem, d],
                 ).start()
 
-    def compute(present, order):
+    def give(c, cut, t):
+        remote(
+            {"expert": t, "dp": lead}, part.at[t, :, cut], ret.at[d, z, :, cut],
+            re_s, re_r.at[c, d],
+        ).start()
+
+    def compute(present, urgent, later):
         for c, cut in enumerate(cuts):
             landed(slots.at[pl.ds(0, present), :, cut], di_r.at[c])
             landed(wgu.at[:, cut, :], w_sem.at[c])
@@ -133,13 +147,13 @@
             landed(wd.at[:, cut], d_sem.at[c])
             made = dot(hidden, wd[:, cut]).astype(jnp.bfloat16)
             part[:, :, cut] = made.reshape(experts, cap, cut.size)
-            for m in order:
-                remote(
-                    {"expert": far[m], "dp": lead}, part.at[far[m], :, cut], ret.at[d, z, :, cut],
-                    re_s, re_r.at[c, d],
-                ).start()
+            for t in urgent:
+                give(c, cut, t)
             if present < experts:
                 ret[lead, z, :, cut] = part[z, :, cut]
+        for c, cut in enumerate(back_cuts):
+            for t in later:
+                give(c, cut, t)
 
     @pl.when(d == lead)
     def _():
@@ -177,7 +191,7 @@
                 if s == lead:
                     slots[z, :, cut] = rows[s, z, :, cut]
 
-        compute(experts - 1, expert_order[:-1])
+        compute(experts - 1, away[:URGENT], away[URGENT:])
 
         for s in range(lead, -1, -1):
             for c, cut in enumerate(back_cuts):
@@ -214,7 +228,7 @@
         pl.semaphore_wait(barrier, 2 * (experts - 1))
         pl.semaphore_signal(go, inc=1, device_id={"dp": lead}, device_id_type=MESH)
 
-        compute(experts, expert_order)
+        compute(experts, away[:URGENT] + [z], away[URGENT:])
 
         landed(tok.at[d], ga_s)
         landed(named.at[d], id_s)
@@ -235,9 +249,9 @@
     dma = pltpu.SemaphoreType.DMA
     shares = pl.pallas_call(
         functools.partial(kernel, groups, experts, sets),
-        out_shape=jax.ShapeDtypeStruct((groups, own, width), bf16),
+        out_shape=pltpu.VMEM((groups, own, width), bf16),
         in_specs=[any_space] * 6,
-        out_specs=any_space,
+        out_specs=pl.BlockSpec(memory_space=pltpu.VMEM),
         scratch_shapes=[
             pltpu.VMEM((sets, groups, own, width), bf16),
             pltpu.VMEM((sets, 2, *expert_ids.shape[:0:-1]), jnp.int32),

time: 25 us -> 23.5 us (0.940)
  other arithmetic: 1.59 us -> 0.69 us
  Pallas kernels: 23.2 us -> 22.7 us
    convert_element_type x1, other arithmetic: 1.59 us -> 0.69 us  [per_device(): return total.astype(bf16)[None]]
    pallas_call x1, Pallas kernels: 23.2 us -> 22.7 us  [per_device(): pl.pallas_call(functools.partial(kernel, groups, experts, sets), out_shap...]
where the time goes in v1:
time: 23.5 us; the launch traced here: 23.4 us
  Pallas kernels  22.7 us (97%)
  other arithmetic  0.69 us (3%)
    pallas_call x1, Pallas kernels, per_device(): pl.pallas_call(functools.partial(kernel, groups, experts, sets), out_shap...  22.7 us
    convert_element_type x1, other arithmetic, per_device(): return total.astype(bf16)[None]  0.69 us

profile of v1, /device:TPU:0, one launch (start us, length us, event | category | flops | bytes accessed | tf_op | source)
XLA Modules:
  0.0 23.4 jit_solution(1149763685231731783)
XLA Ops:
  0.0 22.7 %shard_map.64 = bf16[4,4,7168]{2,1,0:T(4,128)(2,1)S(1)} custom-call(bf16[4,7168]{1,0:T(4,128)(2,1)} %bitcast.13, s32[8,16]{1,0:T(8,128)} %bitcast.14, s32[8,16]{1,0:T(8,128)} %bitcast.15, bf16[7168,512]{1,0:T(8,128)(2,1)} %bitcast.10, bf16[7168,512]{1,0:T(8,128)(2,1)} %bitcast.11, bf16[512,7168]{1,0:T(8,128)(2,1)} %bitcast.12), custom_call_target="tpu_custom_call" | custom-call | tf_op jit(solution)/shard_map/pallas_call | solution.py:250
  22.7 0.7 %add_convert_fusion = bf16[1,4,7168]{2,1,0:T(4,128)(2,1)} fusion(bf16[4,4,7168]{2,1,0:T(4,128)(2,1)S(1)} %shard_map.64), kind=kLoop, calls=%fused_computation | loop fusion | flops 229376 | bytes 286720 | tf_op jit(solution)/shard_map/convert_element_type | solution.py:289

commit v2 on v1

--- a/solution.py
+++ b/solution.py
@@ -8,9 +8,11 @@
 from jax.sharding import PartitionSpec as P
 
 CAPG = 4
-FORWARD = (1, 2, 2, 2)
+FORWARD = (2, 2, 2, 1)
 BACK = (1, 2, 2, 2)
 URGENT = 1
+RELAY = 2
+AFTER = 4
 MESH = pl.DeviceIdType.MESH
 
 
@@ -61,6 +63,17 @@
     return [pl.ds(a, b - a) for a, b in zip(ends[:-1], ends[1:])]
 
 
+def turns(sets, chunks, skip, after):
+    last = sets - 1
+    others = [(s, c) for s in range(last) for c in range(chunks)]
+    return others[:after] + [(last, c) for c in range(skip, chunks)] + others[after:]
+
+
+def relayed(width, groups):
+    ends = [cut.start + cut.size for cut in pieces(width, FORWARD)][:RELAY]
+    return ends[-1] if ends and ends[-1] % (128 * groups) == 0 else 0
+
+
 def partner(a, m, n):
     out, bit = 0, 1
     while bit < n:
@@ -77,8 +90,8 @@
 
 def kernel(
     groups, experts, sets, tokens, ids, codes, w_gate, w_up, w_down, red,
-    tok, named, wgu, wd, rows, slots, acc, part, ret, mixed,
-    tok_sem, in_sem, w_sem, d_sem, id_s, id_r, ga_s, ga_r, di_s, di_r, re_s, re_r, sc_s, sc_r, go,
+    tok, tok_sub, named, wgu, wd, rows, row_sub, hold, slots, acc, part, ret, mixed,
+    tok_sem, in_sem, w_sem, d_sem, id_s, id_r, ga_s, ga_r, di_s, di_r, re_s, re_r, sc_s, sc_r, su_s, su_r, go,
 ):
     g = lax.axis_index("group")
     z = lax.axis_index("expert")
@@ -88,8 +101,13 @@
     cuts = pieces(width, FORWARD)
     back_cuts = pieces(width, BACK)
     cap = CAPG
+    skipped = relayed(width, groups)
+    relay = skipped > 0
+    skip = RELAY if relay else 0
+    sub = skipped // groups
     peer = [partner(g, m, groups) for m in range(groups)]
     far = [partner(z, m, experts) for m in range(experts)]
+    subs = [pl.ds(pl.multiple_of(p * sub, 128), sub) for p in peer] if relay else []
     group_order = list(range(groups - 1, -1, -1))
     expert_order = list(range(experts - 1, -1, -1))
     away = [ends_first(z, k, experts) for k in range(experts - 1)]
@@ -117,11 +135,12 @@
         for c, cut in enumerate(cuts):
             pltpu.make_async_copy(w_gate.at[cut, :], wgu.at[0, cut, :], w_sem.at[c]).start()
             pltpu.make_async_copy(w_up.at[cut, :], wgu.at[1, cut, :], w_sem.at[c]).start()
-        for c, cut in enumerate(back_cuts):
-            pltpu.make_async_copy(w_down.at[:, cut], wd.at[:, cut], d_sem.at[c]).start()
-
-    def send_tokens(order):
-        for cut, sem in zip(cuts, range(len(cuts))):
+        for cut in back_cuts:
+            pltpu.make_async_copy(w_down.at[:, cut], wd.at[:, cut], d_sem).start()
+
+    def send_tokens(which, order):
+        for cut in which:
+            sem = cuts.index(cut)
             for m in order:
                 remote(
                     {"group": peer[m], "dp": lead}, tok.at[d, g, :, cut], tok.at[d, g, :, cut],
@@ -130,27 +149,34 @@
 
     def give(c, cut, t):
         remote(
-            {"expert": t, "dp": lead}, part.at[t, :, cut], ret.at[d, z, :, cut],
-            re_s, re_r.at[c, d],
+            {"expert": t, "dp": lead}, part.at[t, :, cut], ret.at[lead - d, z, :, cut],
+            re_s, re_r.at[c, lead - d],
         ).start()
 
     def compute(present, urgent, later):
-        for c, cut in enumerate(cuts):
-            landed(slots.at[pl.ds(0, present), :, cut], di_r.at[c])
+        line = list(range(len(cuts)))
+        if present == experts:
+            line = line[skip:] + line[:skip]
+        for c in line:
+            cut = cuts[c]
+            if present < experts or c >= skip:
+                landed(slots.at[pl.ds(0, present), :, cut], di_r.at[c])
+            elif c == 0:
+                landed(slots.at[:, :, pl.ds(0, skipped)], su_r.at[2])
             landed(wgu.at[:, cut, :], w_sem.at[c])
             flat = slots[:, :, cut].reshape(experts * cap, cut.size)
             for i in range(2):
                 made = dot(flat, wgu[i, cut, :])
-                acc[i] = made if c == 0 else acc[i] + made
+                acc[i] = made if c == line[0] else acc[i] + made
         hidden = (acc[0] / (1.0 + jnp.exp(-acc[0])) * acc[1]).astype(jnp.bfloat16)
+        landed(wd, d_sem)
         for c, cut in enumerate(back_cuts):
-            landed(wd.at[:, cut], d_sem.at[c])
             made = dot(hidden, wd[:, cut]).astype(jnp.bfloat16)
             part[:, :, cut] = made.reshape(experts, cap, cut.size)
             for t in urgent:
                 give(c, cut, t)
             if present < experts:
-                ret[lead, z, :, cut] = part[z, :, cut]
+                ret[0, z, :, cut] = part[z, :, cut]
         for c, cut in enumerate(back_cuts):
             for t in later:
                 give(c, cut, t)
@@ -167,7 +193,13 @@
         pl.semaphore_wait(barrier, groups - 1 + lead)
         for s in range(lead):
             pl.semaphore_signal(go, inc=1, device_id={"dp": s}, device_id_type=MESH)
-        send_tokens(group_order[:-1])
+        if relay:
+            for m in group_order[:-1]:
+                remote(
+                    {"group": peer[m]}, tok.at[lead, g, :, subs[m]], tok_sub.at[g], ga_s, su_r.at[0]
+                ).start()
+            tok_sub[g] = tok[lead, g, :, subs[0]]
+        send_tokens(cuts[skip:], group_order[:-1])
 
         named_in.wait()
         routes = {lead: routing(named[lead, 0], named[lead, 1], experts, cap)}
@@ -175,43 +207,62 @@
             landed(named.at[s], id_r.at[s])
             routes[s] = routing(named[s, 0], named[s, 1], experts, cap)
 
-        for s in range(lead, -1, -1):
-            for c, cut in enumerate(cuts):
-                landed(tok.at[s, pl.ds(0, groups - 1 if s == lead else groups), :, cut], ga_r.at[c, s])
-                chosen = dot(routes[s][0], tok[s, :, :, cut].reshape(groups * own, cut.size))
-                rows[s, :, :, cut] = chosen.astype(jnp.bfloat16).reshape(experts, cap, cut.size)
-                if (s, c) == (lead, 0):
-                    pl.semaphore_wait(go, lead)
-                for m in expert_order:
-                    if (s, m) != (lead, 0):
-                        remote(
-                            {"expert": far[m], "dp": s}, rows.at[s, far[m], :, cut], slots.at[z, :, cut],
-                            di_s.at[s], di_r.at[c],
-                        ).start()
-                if s == lead:
-                    slots[z, :, cut] = rows[s, z, :, cut]
+        if relay:
+            landed(tok_sub.at[pl.ds(0, groups - 1)], su_r.at[0])
+            chosen = dot(routes[lead][0], tok_sub[...].reshape(groups * own, sub))
+            row_sub[...] = chosen.astype(jnp.bfloat16).reshape(experts, cap, sub)
+        pl.semaphore_wait(go, lead)
+        if relay:
+            for m in expert_order[:-1]:
+                remote({"expert": far[m]}, row_sub.at[far[m]], hold.at[z], su_s.at[0], su_r.at[1]).start()
+            hold[z] = row_sub[z]
+
+        for s, c in turns(sets, len(cuts), skip, AFTER):
+            cut = cuts[c]
+            landed(tok.at[s, pl.ds(0, groups - 1 if s == lead else groups), :, cut], ga_r.at[c, s])
+            chosen = dot(routes[s][0], tok[s, :, :, cut].reshape(groups * own, cut.size))
+            rows[s, :, :, cut] = chosen.astype(jnp.bfloat16).reshape(experts, cap, cut.size)
+            for m in expert_order:
+                if (s, m) != (0, 0):
+                    remote(
+                        {"expert": far[m], "dp": lead - s}, rows.at[s, far[m], :, cut], slots.at[z, :, cut],
+                        di_s.at[s], di_r.at[c],
+                    ).start()
+            if s == 0:
+                slots[z, :, cut] = rows[s, z, :, cut]
+
+        if relay:
+            landed(hold.at[pl.ds(0, experts - 1)], su_r.at[1])
+            for m in group_order:
+                remote(
+                    {"group": peer[m], "dp": 0}, hold, slots.at[:, :, subs[0]], su_s.at[1], su_r.at[2]
+                ).start()
 
         compute(experts - 1, away[:URGENT], away[URGENT:])
 
-        for s in range(lead, -1, -1):
-            for c, cut in enumerate(back_cuts):
-                landed(ret.at[s, pl.ds(0, experts - 1 if s == lead else experts), :, cut], re_r.at[c, s])
-                both = dot(routes[s][1], ret[s, :, :, cut].reshape(experts * cap, cut.size))
-                total = (both[: groups * own] + both[groups * own :]).astype(jnp.bfloat16)
-                mixed[s, :, :, cut] = total.reshape(groups, own, cut.size)
-                for m in group_order:
-                    if (s, m) != (lead, 0):
-                        remote(
-                            {"group": peer[m], "dp": s}, mixed.at[s, peer[m], :, cut], red.at[g, :, cut],
-                            sc_s.at[s], sc_r.at[c],
-                        ).start()
-                if s == lead:
-                    pltpu.make_async_copy(mixed.at[s, g, :, cut], red.at[g, :, cut], sc_r.at[c]).start()
-
-        landed(tok.at[lead, pl.ds(0, groups - 1)], ga_s)
+        for s, c in turns(sets, len(back_cuts), 0, len(back_cuts) * lead):
+            cut = back_cuts[c]
+            landed(ret.at[s, pl.ds(0, experts if s else experts - 1), :, cut], re_r.at[c, s])
+            both = dot(routes[s][1], ret[s, :, :, cut].reshape(experts * cap, cut.size))
+            total = (both[: groups * own] + both[groups * own :]).astype(jnp.bfloat16)
+            mixed[s, :, :, cut] = total.reshape(groups, own, cut.size)
+            for m in group_order:
+                if (s, m) != (lead, 0):
+                    remote(
+                        {"group": peer[m], "dp": s}, mixed.at[s, peer[m], :, cut], red.at[g, :, cut],
+                        sc_s.at[s], sc_r.at[c],
+                    ).start()
+            if s == lead:
+                pltpu.make_async_copy(mixed.at[s, g, :, cut], red.at[g, :, cut], sc_r.at[c]).start()
+
+        if relay:
+            landed(row_sub.at[pl.ds(0, experts - 1)], su_s.at[0])
+            landed(rows.at[lead, :, :, pl.ds(0, skipped)], su_s.at[1])
+        landed(tok.at[lead, pl.ds(0, groups - 1), :, pl.ds(0, width - skipped + sub)], ga_s)
         landed(part.at[pl.ds(0, experts - 1)], re_s)
         for s in range(sets):
-            landed(rows.at[s, pl.ds(0, experts - 1 if s == lead else experts)], di_s.at[s])
+            kept = width - skipped if s == lead else width
+            landed(rows.at[s, pl.ds(0, experts if s else experts - 1), :, pl.ds(0, kept)], di_s.at[s])
             landed(mixed.at[s, pl.ds(0, groups - 1 if s == lead else groups)], sc_s.at[s])
 
     @pl.when(d != lead)
@@ -223,7 +274,7 @@
         tok_in.wait()
         named_in.wait()
         pl.semaphore_wait(go, 1)
-        send_tokens(group_order)
+        send_tokens(cuts, group_order)
         remote({"dp": lead}, named.at[d], named.at[d], id_s, id_r.at[d]).start()
         pl.semaphore_wait(barrier, 2 * (experts - 1))
         pl.semaphore_signal(go, inc=1, device_id={"dp": lead}, device_id_type=MESH)
@@ -245,6 +296,7 @@
     own, width = tokens.shape[1:]
     hid = w_gate.shape[2]
     bf16 = jnp.bfloat16
+    sub = max(128, relayed(width, groups) // groups)
     any_space = pl.BlockSpec(memory_space=pl.ANY)
     dma = pltpu.SemaphoreType.DMA
     shares = pl.pallas_call(
@@ -254,10 +306,13 @@
         out_specs=pl.BlockSpec(memory_space=pltpu.VMEM),
         scratch_shapes=[
             pltpu.VMEM((sets, groups, own, width), bf16),
+            pltpu.VMEM((groups, own, sub), bf16),
             pltpu.VMEM((sets, 2, *expert_ids.shape[:0:-1]), jnp.int32),
             pltpu.VMEM((2, width, hid), bf16),
             pltpu.VMEM((hid, width), bf16),
             pltpu.VMEM((sets, experts, CAPG, width), bf16),
+            pltpu.VMEM((experts, CAPG, sub), bf16),
+            pltpu.VMEM((experts, CAPG, sub), bf16),
             pltpu.VMEM((experts, CAPG, width), bf16),
             pltpu.VMEM((2, experts * CAPG, hid), jnp.float32),
             pltpu.VMEM((experts, CAPG, width), bf16),
@@ -266,7 +321,7 @@
             dma,
             dma,
             dma((len(FORWARD),)),
-            dma((len(BACK),)),
+            dma,
             dma,
             dma((sets - 1,)),
             dma,
@@ -277,6 +332,8 @@
             dma((len(BACK), sets)),
             dma((sets,)),
             dma((len(BACK),)),
+            dma((2,)),
+            dma((3,)),
             pltpu.SemaphoreType.REGULAR,
         ],
         compiler_params=pltpu.CompilerParams(

time: 23.5 us -> 23 us (0.979)
  the two profiles are of different devices: /device:TPU:0 before, /device:TPU:1 now
where the time goes in v2:
time: 23 us; the launch traced here: 22.9 us
  Pallas kernels  22.2 us (97%)
  other arithmetic  0.69 us (3%)
    pallas_call x1, Pallas kernels, per_device(): pl.pallas_call(functools.partial(kernel, groups, experts, sets), out_shap...  22.2 us
    convert_element_type x1, other arithmetic, per_device(): return total.astype(bf16)[None]  0.69 us

profile of v2, /device:TPU:1, one launch (start us, length us, event | category | flops | bytes accessed | tf_op | source)
XLA Modules:
  0.0 22.9 jit_solution(11212917933488182705)
XLA Ops:
  0.0 22.2 %shard_map.64 = bf16[4,4,7168]{2,1,0:T(4,128)(2,1)S(1)} custom-call(bf16[4,7168]{1,0:T(4,128)(2,1)} %bitcast.13, s32[8,16]{1,0:T(8,128)} %bitcast.14, s32[8,16]{1,0:T(8,128)} %bitcast.15, bf16[7168,512]{1,0:T(8,128)(2,1)} %bitcast.10, bf16[7168,512]{1,0:T(8,128)(2,1)} %bitcast.11, bf16[512,7168]{1,0:T(8,128)(2,1)} %bitcast.12), custom_call_target="tpu_custom_call" | custom-call | tf_op jit(solution)/shard_map/pallas_call | solution.py:302
  22.2 0.7 %add_convert_fusion = bf16[1,4,7168]{2,1,0:T(4,128)(2,1)} fusion(bf16[4,4,7168]{2,1,0:T(4,128)(2,1)S(1)} %shard_map.64), kind=kLoop, calls=%fused_computation | loop fusion | flops 229376 | bytes 286720 | tf_op jit(solution)/shard_map/convert_element_type | solution.py:346

commit v3 on v2

--- a/solution.py
+++ b/solution.py
@@ -9,7 +9,7 @@
 
 CAPG = 4
 FORWARD = (2, 2, 2, 1)
-BACK = (1, 2, 2, 2)
+BACK = (1, 1, 1, 1)
 URGENT = 1
 RELAY = 2
 AFTER = 4
@@ -170,9 +170,12 @@
                 acc[i] = made if c == line[0] else acc[i] + made
         hidden = (acc[0] / (1.0 + jnp.exp(-acc[0])) * acc[1]).astype(jnp.bfloat16)
         landed(wd, d_sem)
+        made = dot(hidden, wd[:, back_cuts[0]])
         for c, cut in enumerate(back_cuts):
-            made = dot(hidden, wd[:, cut]).astype(jnp.bfloat16)
-            part[:, :, cut] = made.reshape(experts, cap, cut.size)
+            ready = made.astype(jnp.bfloat16)
+            if c + 1 < len(back_cuts):
+                made = dot(hidden, wd[:, back_cuts[c + 1]])
+            part[:, :, cut] = ready.reshape(experts, cap, cut.size)
             for t in urgent:
                 give(c, cut, t)
             if present < experts:
@@ -238,7 +241,7 @@
                     {"group": peer[m], "dp": 0}, hold, slots.at[:, :, subs[0]], su_s.at[1], su_r.at[2]
                 ).start()
 
-        compute(experts - 1, away[:URGENT], away[URGENT:])
+        compute(experts - 1, away, [])
 
         for s, c in turns(sets, len(back_cuts), 0, len(back_cuts) * lead):
             cut = back_cuts[c]

time: 23 us -> 23 us (level)
  no operation moved by 1% of the time
where the time goes in v3:
time: 23 us; the launch traced here: 22.8 us
  Pallas kernels  22.2 us (97%)
  other arithmetic  0.69 us (3%)
    pallas_call x1, Pallas kernels, per_device(): pl.pallas_call(functools.partial(kernel, groups, experts, sets), out_shap...  22.2 us
    convert_element_type x1, other arithmetic, per_device(): return total.astype(bf16)[None]  0.69 us

profile of v3, /device:TPU:1, one launch (start us, length us, event | category | flops | bytes accessed | tf_op | source)
XLA Modules:
  0.0 22.8 jit_solution(7061783727343507669)
XLA Ops:
  0.0 22.2 %shard_map.64 = bf16[4,4,7168]{2,1,0:T(4,128)(2,1)S(1)} custom-call(bf16[4,7168]{1,0:T(4,128)(2,1)} %bitcast.13, s32[8,16]{1,0:T(8,128)} %bitcast.14, s32[8,16]{1,0:T(8,128)} %bitcast.15, bf16[7168,512]{1,0:T(8,128)(2,1)} %bitcast.10, bf16[7168,512]{1,0:T(8,128)(2,1)} %bitcast.11, bf16[512,7168]{1,0:T(8,128)(2,1)} %bitcast.12), custom_call_target="tpu_custom_call" | custom-call | tf_op jit(solution)/shard_map/pallas_call | solution.py:305
  22.2 0.7 %add_convert_fusion = bf16[1,4,7168]{2,1,0:T(4,128)(2,1)} fusion(bf16[4,4,7168]{2,1,0:T(4,128)(2,1)S(1)} %shard_map.64), kind=kLoop, calls=%fused_computation | loop fusion | flops 229376 | bytes 286720 | tf_op jit(solution)/shard_map/convert_element_type | solution.py:349

commit v4 on v3

--- a/solution.py
+++ b/solution.py
@@ -89,8 +89,8 @@
 
 
 def kernel(
-    groups, experts, sets, tokens, ids, codes, w_gate, w_up, w_down, red,
-    tok, tok_sub, named, wgu, wd, rows, row_sub, hold, slots, acc, part, ret, mixed,
+    groups, experts, sets, tokens, ids, codes, w_gate, w_up, w_down, out,
+    red, tok, tok_sub, named, wgu, wd, rows, row_sub, hold, slots, acc, part, ret, mixed,
     tok_sem, in_sem, w_sem, d_sem, id_s, id_r, ga_s, ga_r, di_s, di_r, re_s, re_r, sc_s, sc_r, su_s, su_r, go,
 ):
     g = lax.axis_index("group")
@@ -132,9 +132,9 @@
         pltpu.make_async_copy(ref, ref, sem).wait()
 
     def load():
-        for c, cut in enumerate(cuts):
-            pltpu.make_async_copy(w_gate.at[cut, :], wgu.at[0, cut, :], w_sem.at[c]).start()
-            pltpu.make_async_copy(w_up.at[cut, :], wgu.at[1, cut, :], w_sem.at[c]).start()
+        for cut in cuts:
+            pltpu.make_async_copy(w_gate.at[cut, :], wgu.at[0, cut, :], w_sem).start()
+            pltpu.make_async_copy(w_up.at[cut, :], wgu.at[1, cut, :], w_sem).start()
         for cut in back_cuts:
             pltpu.make_async_copy(w_down.at[:, cut], wd.at[:, cut], d_sem).start()
 
@@ -163,7 +163,8 @@
                 landed(slots.at[pl.ds(0, present), :, cut], di_r.at[c])
             elif c == 0:
                 landed(slots.at[:, :, pl.ds(0, skipped)], su_r.at[2])
-            landed(wgu.at[:, cut, :], w_sem.at[c])
+            if c == line[0]:
+                landed(wgu, w_sem)
             flat = slots[:, :, cut].reshape(experts * cap, cut.size)
             for i in range(2):
                 made = dot(flat, wgu[i, cut, :])
@@ -290,6 +291,10 @@
 
     for c, cut in enumerate(back_cuts):
         landed(red.at[:, :, cut], sc_r.at[c])
+        total = red[0, :, cut].astype(jnp.float32)
+        for k in range(1, groups):
+            total = total + red[k, :, cut].astype(jnp.float32)
+        out[:, cut] = total.astype(out.dtype)
 
 
 def per_device(tokens, expert_ids, gate_codes, w_gate, w_up, w_down):
@@ -302,12 +307,13 @@
     sub = max(128, relayed(width, groups) // groups)
     any_space = pl.BlockSpec(memory_space=pl.ANY)
     dma = pltpu.SemaphoreType.DMA
-    shares = pl.pallas_call(
+    return pl.pallas_call(
         functools.partial(kernel, groups, experts, sets),
-        out_shape=pltpu.VMEM((groups, own, width), bf16),
+        out_shape=pltpu.VMEM((own, width), bf16),
         in_specs=[any_space] * 6,
         out_specs=pl.BlockSpec(memory_space=pltpu.VMEM),
         scratch_shapes=[
+            pltpu.VMEM((groups, own, width), bf16),
             pltpu.VMEM((sets, groups, own, width), bf16),
             pltpu.VMEM((groups, own, sub), bf16),
             pltpu.VMEM((sets, 2, *expert_ids.shape[:0:-1]), jnp.int32),
@@ -323,7 +329,7 @@
             pltpu.VMEM((sets, groups, own, width), bf16),
             dma,
             dma,
-            dma((len(FORWARD),)),
+            dma,
             dma,
             dma,
             dma((sets - 1,)),
@@ -342,11 +348,7 @@
         compiler_params=pltpu.CompilerParams(
             collective_id=0, has_side_effects=True, vmem_limit_bytes=60 * 1024 * 1024
         ),
-    )(tokens[0], expert_ids[0].T, gate_codes[0].T, w_gate[0], w_up[0], w_down[0])
-    total = shares[0].astype(jnp.float32)
-    for k in range(1, groups):
-        total = total + shares[k].astype(jnp.float32)
-    return total.astype(bf16)[None]
+    )(tokens[0], expert_ids[0].T, gate_codes[0].T, w_gate[0], w_up[0], w_down[0])[None]
 
 
 def solution(mesh):

time: 23 us -> 22.9 us (level)
  other arithmetic: 0.69 us -> 0 us
  local copies, waits for them, and re-layouts: 0 us -> 0.63 us
    convert_element_type x1 -> x0, other arithmetic: 0.69 us -> none  [per_device(): return total.astype(bf16)[None]]
    unnamed x0 -> x1, local copies, waits for them, and re-layouts: none -> 0.63 us
where the time goes in v4:
time: 22.9 us; the launch traced here: 22.8 us
  Pallas kernels  22.1 us (97%)
  local copies, waits for them, and re-layouts  0.63 us (3%)
    pallas_call x1, Pallas kernels, per_device(): pl.pallas_call(functools.partial(kernel, groups, experts, sets), out_shap...  22.1 us
    unnamed x1, local copies, waits for them, and re-layouts  0.63 us

profile of v4, /device:TPU:1, one launch (start us, length us, event | category | flops | bytes accessed | tf_op | source)
XLA Modules:
  0.0 22.8 jit_solution(3094736662348253408)
XLA Ops:
  0.0 22.1 %shard_map.64 = bf16[4,7168]{1,0:T(4,128)(2,1)S(1)} custom-call(bf16[4,7168]{1,0:T(4,128)(2,1)} %bitcast.15, s32[8,16]{1,0:T(8,128)} %bitcast.16, s32[8,16]{1,0:T(8,128)} %bitcast.17, bf16[7168,512]{1,0:T(8,128)(2,1)} %bitcast.12, bf16[7168,512]{1,0:T(8,128)(2,1)} %bitcast.13, bf16[512,7168]{1,0:T(8,128)(2,1)} %bitcast.14), custom_call_target="tpu_custom_call" | custom-call | tf_op jit(solution)/shard_map/pallas_call | solution.py:310
  22.1 0.6 %copy.8 = bf16[1,4,7168]{2,1,0:T(4,128)(2,1)} copy(bf16[1,4,7168]{2,1,0:T(4,128)(2,1)S(1)} %bitcast.11) | data formatting | bytes 114688
